TPU v7x, 32 devices: a whole 2x2x4 slice. The times are simulated.
32 devices in a mesh: fsdp: 4 (over x, core), vocab: 8 (over z, y).
Axes of the slice: x: 2, y: 2, z: 4, core: 2. Of those that a mesh axis runs over, the one named last changes fastest.
Arguments:
- hidden_states: bfloat16 [512, 3072], P('fsdp', 'vocab'), may hold values from -512 to 512
- head: bfloat16 [3072, 16384], P('fsdp', 'vocab'), may hold values from -0.25259074 to 0.25259074
- labels: int32 [512], P('fsdp'), may hold values from 0 to 16383
Outputs:
- token_loss: float32 [512], P('fsdp')
- state_grad: bfloat16 [512, 3072], P('fsdp', 'vocab')
- head_grad: float32 [3072, 16384], P('fsdp', 'vocab')
All inputs are finite; a program needn't handle non-finite values.
Results may differ from a plain program's by a relative error of at most 0.0034.
Values may be sent and summed in bfloat16 or wider, within the bound.
A program may use at most 128 MiB of HBM per device.

v0:
```python
import jax
import jax.numpy as jnp
from jax import lax
from jax.sharding import PartitionSpec as P


def local(hidden_states, head, labels):
    features = lax.all_gather(hidden_states, "vocab", axis=1, tiled=True)
    weights = lax.all_gather(head, "fsdp", axis=0, tiled=True)
    logits = jnp.dot(features, weights, preferred_element_type=jnp.float32)
    width = weights.shape[1]
    columns = lax.axis_index("vocab") * width + jnp.arange(width, dtype=jnp.int32)
    hits = labels[:, None] == columns[None, :]
    local_target = jnp.sum(jnp.where(hits, logits, jnp.float32(0.0)), axis=1)
    local_peak = jnp.max(logits, axis=1)
    peak = lax.pmax(local_peak, "vocab")
    shifted = jnp.exp(logits - peak[:, None])
    total, target = lax.psum((jnp.sum(shifted, axis=1), local_target), "vocab")
    token_loss = jnp.log(total) + peak - target
    errors = (shifted / total[:, None] - hits.astype(jnp.float32)).astype(jnp.bfloat16)
    state_terms = lax.dot_general(
        errors, weights, (((1,), (1,)), ((), ())), preferred_element_type=jnp.float32
    )
    state_grad = lax.psum_scatter(state_terms, "vocab", scatter_dimension=1, tiled=True).astype(
        jnp.bfloat16
    )
    all_errors = lax.all_gather(errors, "fsdp", axis=0, tiled=True)
    slices = lax.all_to_all(features, "fsdp", split_axis=1, concat_axis=0, tiled=True)
    head_grad = lax.dot_general(
        slices, all_errors, (((0,), (0,)), ((), ())), preferred_element_type=jnp.float32
    )
    return (token_loss, state_grad, head_grad)


def solution(mesh):
    in_specs = (P("fsdp", "vocab"), P("fsdp", "vocab"), P("fsdp"))
    out_specs = (P("fsdp"), P("fsdp", "vocab"), P("fsdp", "vocab"))
    return jax.shard_map(local, mesh=mesh, in_specs=in_specs, out_specs=out_specs, check_vma=False)
```

profile of v0, /device:TPU:0, one launch (start us, length us, event | category | flops | bytes accessed | tf_op | source)
XLA Modules:
  0.0 245.0 jit_solution(18237512961004457685)
XLA Ops:
  7.2 0.0 all-gather.3.cloned.1.call-start
  7.2 0.7 all-gather.3.cloned.1.call-update
  7.9 0.0 all-gather.5.cloned.1.call-start
  7.9 1.0 copy.8
  9.0 33.9 %all_gather.9 = bf16[128,3072]{0,1:T(8,128)(2,1)S(1)} all-gather(bf16[128,384]{0,1:T(8,128)(2,1)S(1)} %copy.8), channel_id=1, replica_groups=mesh['fsdp'=4,'vocab'=8] {'vocab'}, dimensions={1}, use_global_device_ids=true | all-gather | bytes 884736 | tf_op jit(solution)/shard_map/all_gather | solution.py:8
  42.9 0.0 copy-start
  42.9 51.5 %all-gather.3.cloned.1.call-done = bf16[3072,2048]{1,0:T(8,128)(2,1)} async-done(((bf16[768,2048]{1,0:T(8,128)(2,1)}), bf16[3072,2048]{1,0:T(8,128)(2,1)}) %all-gather.3.cloned.1.call-update) | async-done | bytes 12582928 | tf_op jit(solution)/shard_map/all_gather | solution.py:9
  94.4 6.5 %fusion.4 = (f32[128]{0:T(128)S(1)}, f32[128,2048]{1,0:T(8,128)S(1)}) fusion(bf16[128,3072]{0,1:T(8,128)(2,1)S(1)} %all_gather.9, bf16[3072,2048]{1,0:T(8,128)(2,1)} %all-gather.3.cloned.1.call-done), kind=kOutput, calls=%fused_computation.10 | convolution fusion | flops 1610874752 | bytes 14418432 | tf_op jit(solution)/shard_map/dot_general | solution.py:10
  100.8 21.4 %pmax.7 = f32[128]{0:T(128)S(1)} all-reduce(f32[128]{0:T(128)S(1)} %get-tuple-element.16), channel_id=1, replica_groups=mesh['fsdp'=4,'vocab'=8] {'vocab'}, use_global_device_ids=true, to_apply=%region_1.2 | all-reduce | flops 128 | bytes 1024 | tf_op jit(solution)/shard_map/pmax | solution.py:16
  122.2 0.0 copy-done
  122.2 0.4 fusion.3
  122.6 17.1 %all-reduce = (f32[128]{0:T(128)S(1)}, f32[128]{0:T(128)S(1)}) all-reduce(f32[128]{0:T(128)S(1)} %get-tuple-element.13, f32[128]{0:T(128)S(1)} %get-tuple-element.12), channel_id=1, replica_groups=mesh['fsdp'=4,'vocab'=8] {'vocab'}, use_global_device_ids=true, to_apply=%region_5.6 | all-reduce | flops 256 | bytes 2048 | tf_op jit(solution)/shard_map/psum | solution.py:18
  139.7 1.2 fusion.2
  140.9 0.0 all-gather.5.cloned.1.call-update
  140.9 0.0 reduce-scatter.2.cloned.1.call-start
  141.0 10.4 %fusion.5 = f32[128,3072]{1,0:T(8,128)} fusion(bf16[128,2048]{1,0:T(8,128)(2,1)} %fusion.2, bf16[3072,2048]{1,0:T(8,128)(2,1)} %all-gather.3.cloned.1.call-done), kind=kOutput, calls=%fused_computation.11 | convolution fusion | flops 1610612736 | bytes 14680064 | tf_op jit(solution)/shard_map/dot_general | solution.py:21
  151.3 0.0 reduce-scatter.2.cloned.1.call-update
  151.4 16.9 %all_to_all.19 = bf16[128,4,768]{0,2,1:T(8,128)(2,1)S(1)} all-to-all(bf16[128,4,768]{0,2,1:T(8,128)(2,1)S(1)} %bitcast.11), channel_id=1, replica_groups=mesh['fsdp'=4,'vocab'=8] {'fsdp'}, dimensions={1} | all-to-all | bytes 1572864 | tf_op jit(solution)/shard_map/all_to_all | solution.py:28
  168.3 0.3 copy.9
  168.6 0.5 add_subtract_fusion
  169.1 0.0 all-gather.5.cloned.1.call-done
  169.1 6.1 %convolution_bitcast_fusion = f32[768,2048]{0,1:T(8,128)} fusion(bf16[512,2048]{1,0:T(8,128)(2,1)} %all-gather.5.cloned.1.call-done, bf16[512,768]{1,0:T(8,128)(2,1)S(1)} %bitcast.12), kind=kOutput, calls=%fused_computation | convolution fusion | flops 1610612736 | bytes 9175040 | tf_op jit(solution)/shard_map/dot_general | solution.py:29
  175.2 6.6 %copy.10 = f32[768,2048]{1,0:T(8,128)} copy(f32[768,2048]{0,1:T(8,128)} %convolution_bitcast_fusion) | data formatting | bytes 12582912
  181.8 55.1 %reduce-scatter.2.cloned.1.call-done = f32[128,384]{1,0:T(8,128)} async-done(((f32[128,3072]{1,0:T(8,128)}), f32[128,384]{1,0:T(8,128)}) %reduce-scatter.2.cloned.1.call-update) | async-done | bytes 196624 | tf_op jit(solution)/shard_map/reduce_scatter | solution.py:24
  236.9 1.6 convert_element_type.11
  (1 shorter events, 0.0 us)
Async XLA Ops:
  7.2 87.2 %all-gather.3.cloned.1.call-start = ((), (), s32[]{:S(2)}) async-start(), calls=%async_computation.2 | async-start | bytes 15728640 | tf_op jit(solution)/shard_map/all_gather | solution.py:9
  7.9 161.2 %all-gather.5.cloned.1.call-start = ((), (), s32[]{:S(2)}) async-start(), calls=%async_computation.4 | async-start | bytes 2621440 | tf_op jit(solution)/shard_map/all_gather | solution.py:27
  42.9 79.3 %copy-start = (s32[128]{0:T(128)S(1)}, s32[128]{0:T(128)}, u32[]{:S(2)}) copy-start(s32[128]{0:T(128)} %param.5) | copy-start | bytes 1540
  140.9 96.0 %reduce-scatter.2.cloned.1.call-start = ((), (), s32[]{:S(2)}) async-start(), calls=%async_computation.3 | async-start | bytes 1769472 | tf_op jit(solution)/shard_map/reduce_scatter | solution.py:24
Sparse Core Ops, SparseCore 0:
  9.5 84.7 all-gather.2
  141.0 23.2 all-gather.4
  167.8 69.0 reduce-scatter.1
where the time goes:
time: 245 us
  waiting for transfers between devices  107 us (44%)
  blocking collectives  89.3 us (36%)
  matrix products  22.9 us (9%)
  between operations  13.8 us (6%)
  local copies, waits for them, and re-layouts  7.87 us (3%)
  other arithmetic  3.66 us (1%)
    reduce_scatter x1, waiting for transfers between devices, local(): lax.psum_scatter(state_terms, 'vocab', scatter_dimension=1, tiled=True)  55.1 us
    all_gather x1, waiting for transfers between devices, local(): weights = lax.all_gather(head, 'fsdp', axis=0, tiled=True)  51.5 us
    all_gather x1, blocking collectives, local(): features = lax.all_gather(hidden_states, 'vocab', axis=1, tiled=True)  33.9 us
    pmax x1, blocking collectives, local(): peak = lax.pmax(local_peak, 'vocab')  21.4 us
    psum x1, blocking collectives, local(): total, target = lax.psum((jnp.sum(shifted, axis=1), local_target), 'vocab')  17.1 us
    all_to_all x1, blocking collectives, local(): lax.all_to_all(features, 'fsdp', split_axis=1, concat_axis=0, tiled=True)  16.9 us
    dot_general x1, matrix products, local(): lax.dot_general(errors, weights, (((1,), (1,)), ((), ())), preferred_elem...  10.4 us
    unnamed x4, local copies, waits for them, and re-layouts  7.59 us
  transfers between devices with their start and end apart: 3, of which 2 were waited for; matrix products, arithmetic and copies ran while one was open for 10% of the time, Pallas kernels for 0%

commit v1 on v0

--- a/solution.py
+++ b/solution.py
@@ -5,7 +5,14 @@
 
 
 def local(hidden_states, head, labels):
-    features = lax.all_gather(hidden_states, "vocab", axis=1, tiled=True)
+    ring = [hidden_states]
+    for hop in range(7):
+        ring.append(lax.ppermute(ring[-1], "vocab", [(dev, (dev + 1) % 8) for dev in range(8)]))
+    features = jnp.roll(
+        jnp.concatenate(ring[::-1], axis=1),
+        (lax.axis_index("vocab") + 1) * ring[0].shape[1],
+        axis=1,
+    )
     weights = lax.all_gather(head, "fsdp", axis=0, tiled=True)
     logits = jnp.dot(features, weights, preferred_element_type=jnp.float32)
     width = weights.shape[1]

time: 245 us -> 250 us (1.020)
  waiting for transfers between devices: 107 us -> 154 us
  blocking collectives: 89.3 us -> 52.5 us
  local copies, waits for them, and re-layouts: 7.87 us -> 0.97 us
  starting transfers between devices: 0.12 us -> 3.18 us
    ppermute x0 -> x7, waiting for transfers between devices: none -> 50.6 us  [local(): lax.ppermute(ring[-1], 'vocab', [(dev, (dev + 1) % 8) for dev in range(8)])]
    all_gather x1 -> x0, blocking collectives: 33.9 us -> none  [local(): features = lax.all_gather(hidden_states, 'vocab', axis=1, tiled=True)]
    all_gather x1, waiting for transfers between devices: 0.01 us -> 21.4 us  [local(): all_errors = lax.all_gather(errors, 'fsdp', axis=0, tiled=True)]
    all_gather x1, waiting for transfers between devices: 51.5 us -> 31.9 us  [local(): weights = lax.all_gather(head, 'fsdp', axis=0, tiled=True)]
    unnamed x4 -> x22, local copies, waits for them, and re-layouts: 7.59 us -> 0.46 us
    reduce_scatter x1, waiting for transfers between devices: 55.1 us -> 48.2 us  [local(): lax.psum_scatter(state_terms, 'vocab', scatter_dimension=1, tiled=True)]
    ppermute x0 -> x7, starting transfers between devices: none -> 3.06 us  [local(): lax.ppermute(ring[-1], 'vocab', [(dev, (dev + 1) % 8) for dev in range(8)])]
    all_to_all x1, blocking collectives: 16.9 us -> 14 us  [local(): lax.all_to_all(features, 'fsdp', split_axis=1, concat_axis=0, tiled=True)]
  transfers between devices with their start and end apart: 3 -> 10, of which waited for: 2 -> 10; matrix products, arithmetic and copies ran while one was open for 10% -> 1% of each run, Pallas kernels for 0% -> 0%
where the time goes in v1:
time: 250 us
  waiting for transfers between devices  154 us (62%)
  blocking collectives  52.5 us (21%)
  matrix products  22.7 us (9%)
  between operations  13.9 us (6%)
  starting transfers between devices  3.18 us (1%)
  other arithmetic  2.87 us (1%)
    ppermute x7, waiting for transfers between devices, local(): lax.ppermute(ring[-1], 'vocab', [(dev, (dev + 1) % 8) for dev in range(8)])  50.6 us
    reduce_scatter x1, waiting for transfers between devices, local(): lax.psum_scatter(state_terms, 'vocab', scatter_dimension=1, tiled=True)  48.2 us
    all_gather x1, waiting for transfers between devices, local(): weights = lax.all_gather(head, 'fsdp', axis=0, tiled=True)  31.9 us
    all_gather x1, waiting for transfers between devices, local(): all_errors = lax.all_gather(errors, 'fsdp', axis=0, tiled=True)  21.4 us
    pmax x1, blocking collectives, local(): peak = lax.pmax(local_peak, 'vocab')  21.4 us
    psum x1, blocking collectives, local(): total, target = lax.psum((jnp.sum(shifted, axis=1), local_target), 'vocab')  17.1 us
    all_to_all x1, blocking collectives, local(): lax.all_to_all(features, 'fsdp', split_axis=1, concat_axis=0, tiled=True)  14 us
    dot_general x1, matrix products, local(): lax.dot_general(errors, weights, (((1,), (1,)), ((), ())), preferred_elem...  10.1 us
  transfers between devices with their start and end apart: 10, of which 10 were waited for; matrix products, arithmetic and copies ran while one was open for 1% of the time, Pallas kernels for 0%

profile of v1, /device:TPU:0, one launch (start us, length us, event | category | flops | bytes accessed | tf_op | source)
XLA Modules:
  0.0 249.7 jit_solution(7690677468839503939)
XLA Ops:
  7.2 0.0 copy-start.1
  7.2 0.0 all-gather.3.cloned.1.call-start
  7.2 0.7 all-gather.3.cloned.1.call-update
  7.9 0.0 reduce-scatter.2.cloned.1.call-start
  8.0 0.1 copy-done.1
  8.1 0.1 copy.6
  8.2 3.0 %collective-permute-start = (bf16[128,384]{0,1:T(8,128)(2,1)S(1)}, bf16[128,384]{0,1:T(8,128)(2,1)S(1)}, u32[]{:S(2)}, u32[]{:S(2)}) collective-permute-start(bf16[128,384]{0,1:T(8,128)(2,1)S(1)} %copy.6), channel_id=1, source_target_pairs={{0,1},{1,2},{2,3},{3,4},{4,5},{5,6},{6,7},{7,0},{8,9},{9,10},{10,1... | collective-permute-start | bytes 294920 | tf_op jit(solution)/shard_map/ppermute | solution.py:10
  11.2 5.8 %collective-permute-done = bf16[128,384]{0,1:T(8,128)(2,1)S(1)} collective-permute-done((bf16[128,384]{0,1:T(8,128)(2,1)S(1)}, bf16[128,384]{0,1:T(8,128)(2,1)S(1)}, u32[]{:S(2)}, u32[]{:S(2)}) %collective-permute-start) | collective-permute-done | bytes 98336 | tf_op jit(solution)/shard_map/ppermute | solution.py:10
  17.1 0.0 collective-permute-start.1
  17.1 7.3 %collective-permute-done.1 = bf16[128,384]{0,1:T(8,128)(2,1)S(1)} collective-permute-done((bf16[128,384]{0,1:T(8,128)(2,1)S(1)}, bf16[128,384]{0,1:T(8,128)(2,1)S(1)}, u32[]{:S(2)}, u32[]{:S(2)}) %collective-permute-start.1) | collective-permute-done | bytes 98336 | tf_op jit(solution)/shard_map/ppermute | solution.py:10
  24.4 0.0 collective-permute-start.2
  24.4 7.3 %collective-permute-done.2 = bf16[128,384]{0,1:T(8,128)(2,1)S(1)} collective-permute-done((bf16[128,384]{0,1:T(8,128)(2,1)S(1)}, bf16[128,384]{0,1:T(8,128)(2,1)S(1)}, u32[]{:S(2)}, u32[]{:S(2)}) %collective-permute-start.2) | collective-permute-done | bytes 98336 | tf_op jit(solution)/shard_map/ppermute | solution.py:10
  31.7 0.0 collective-permute-start.3
  31.7 7.3 %collective-permute-done.3 = bf16[128,384]{0,1:T(8,128)(2,1)S(1)} collective-permute-done((bf16[128,384]{0,1:T(8,128)(2,1)S(1)}, bf16[128,384]{0,1:T(8,128)(2,1)S(1)}, u32[]{:S(2)}, u32[]{:S(2)}) %collective-permute-start.3) | collective-permute-done | bytes 98336 | tf_op jit(solution)/shard_map/ppermute | solution.py:10
  39.0 0.0 collective-permute-start.4
  39.0 7.4 %collective-permute-done.4 = bf16[128,384]{0,1:T(8,128)(2,1)S(1)} collective-permute-done((bf16[128,384]{0,1:T(8,128)(2,1)S(1)}, bf16[128,384]{0,1:T(8,128)(2,1)S(1)}, u32[]{:S(2)}, u32[]{:S(2)}) %collective-permute-start.4) | collective-permute-done | bytes 98336 | tf_op jit(solution)/shard_map/ppermute | solution.py:10
  46.4 0.0 collective-permute-start.5
  46.4 8.2 %collective-permute-done.5 = bf16[128,384]{0,1:T(8,128)(2,1)S(1)} collective-permute-done((bf16[128,384]{0,1:T(8,128)(2,1)S(1)}, bf16[128,384]{0,1:T(8,128)(2,1)S(1)}, u32[]{:S(2)}, u32[]{:S(2)}) %collective-permute-start.5) | collective-permute-done | bytes 98336 | tf_op jit(solution)/shard_map/ppermute | solution.py:10
  54.6 0.0 collective-permute-start.6
  54.6 7.3 %collective-permute-done.6 = bf16[128,384]{0,1:T(8,128)(2,1)S(1)} collective-permute-done((bf16[128,384]{0,1:T(8,128)(2,1)S(1)}, bf16[128,384]{0,1:T(8,128)(2,1)S(1)}, u32[]{:S(2)}, u32[]{:S(2)}) %collective-permute-start.6) | collective-permute-done | bytes 98336 | tf_op jit(solution)/shard_map/ppermute | solution.py:10
  62.3 0.2 constant_dynamic-slice_fusion
  62.5 0.0 copy-start.2
  62.5 31.9 %all-gather.3.cloned.1.call-done = bf16[3072,2048]{1,0:T(8,128)(2,1)} async-done(((bf16[768,2048]{1,0:T(8,128)(2,1)}), bf16[3072,2048]{1,0:T(8,128)(2,1)}) %all-gather.3.cloned.1.call-update) | async-done | bytes 12582928 | tf_op jit(solution)/shard_map/all_gather | solution.py:16
  94.4 6.5 %fusion.4 = (f32[128]{0:T(128)S(1)}, f32[128,2048]{1,0:T(8,128)S(1)}) fusion(bf16[128,3072]{0,1:T(8,128)(2,1)S(1)} %constant_dynamic-slice_fusion, bf16[3072,2048]{1,0:T(8,128)(2,1)} %all-gather.3.cloned.1.call-done), kind=kOutput, calls=%fused_computation.26 | convolution fusion | flops 1610874752 | bytes 14418432 | tf_op jit(solution)/shard_map/dot_general | solution.py:17
  100.8 21.4 %pmax.7 = f32[128]{0:T(128)S(1)} all-reduce(f32[128]{0:T(128)S(1)} %get-tuple-element.7), channel_id=1, replica_groups=mesh['fsdp'=4,'vocab'=8] {'vocab'}, use_global_device_ids=true, to_apply=%region_1.2 | all-reduce | flops 128 | bytes 1024 | tf_op jit(solution)/shard_map/pmax | solution.py:23
  122.2 0.0 copy-done.2
  122.2 0.4 fusion.3
  122.6 17.1 %all-reduce = (f32[128]{0:T(128)S(1)}, f32[128]{0:T(128)S(1)}) all-reduce(f32[128]{0:T(128)S(1)} %get-tuple-element.4, f32[128]{0:T(128)S(1)} %get-tuple-element.3), channel_id=1, replica_groups=mesh['fsdp'=4,'vocab'=8] {'vocab'}, use_global_device_ids=true, to_apply=%region_5.6 | all-reduce | flops 256 | bytes 2048 | tf_op jit(solution)/shard_map/psum | solution.py:25
  139.7 0.4 fusion.2
  140.1 0.0 copy-start
  140.1 10.1 %fusion.5 = f32[128,3072]{1,0:T(8,128)} fusion(bf16[128,2048]{1,0:T(8,128)(2,1)S(1)} %fusion.2, bf16[3072,2048]{1,0:T(8,128)(2,1)} %all-gather.3.cloned.1.call-done), kind=kOutput, calls=%fused_computation.27 | convolution fusion | flops 1610612736 | bytes 14680064 | tf_op jit(solution)/shard_map/dot_general | solution.py:28
  150.3 0.0 copy-done
  150.3 0.0 reduce-scatter.2.cloned.1.call-update
  150.3 0.0 all-gather.5.cloned.1.call-start
  150.3 0.7 all-gather.5.cloned.1.call-update
  151.0 14.0 %all_to_all.19 = bf16[128,4,768]{0,2,1:T(8,128)(2,1)S(1)} all-to-all(bf16[128,4,768]{0,2,1:T(8,128)(2,1)S(1)} %bitcast.9), channel_id=1, replica_groups=mesh['fsdp'=4,'vocab'=8] {'fsdp'}, dimensions={1} | all-to-all | bytes 1572864 | tf_op jit(solution)/shard_map/all_to_all | solution.py:35
  165.1 0.3 copy.9
  165.4 0.5 add_subtract_fusion
  165.9 48.2 %reduce-scatter.2.cloned.1.call-done = f32[128,384]{1,0:T(8,128)} async-done(((f32[128,3072]{1,0:T(8,128)}), f32[128,384]{1,0:T(8,128)}) %reduce-scatter.2.cloned.1.call-update) | async-done | bytes 196624 | tf_op jit(solution)/shard_map/reduce_scatter | solution.py:31
  214.1 1.6 convert_element_type.11
  215.7 21.4 %all-gather.5.cloned.1.call-done = bf16[512,2048]{1,0:T(8,128)(2,1)} async-done(((bf16[128,2048]{1,0:T(8,128)(2,1)}), bf16[512,2048]{1,0:T(8,128)(2,1)}) %all-gather.5.cloned.1.call-update) | async-done | bytes 2097168 | tf_op jit(solution)/shard_map/all_gather | solution.py:34
  237.1 6.1 %fusion.6 = f32[768,2048]{1,0:T(8,128)} fusion(bf16[512,768]{1,0:T(8,128)(2,1)S(1)} %bitcast.10, bf16[512,2048]{1,0:T(8,128)(2,1)} %all-gather.5.cloned.1.call-done), kind=kOutput, calls=%fused_computation.28 | convolution fusion | flops 1610612736 | bytes 9175040 | tf_op jit(solution)/shard_map/dot_general | solution.py:36
  (17 shorter events, 0.2 us)
Async XLA Ops:
  7.2 0.9 copy-start.1
  7.2 87.2 %all-gather.3.cloned.1.call-start = ((), (), s32[]{:S(2)}) async-start(), calls=%async_computation.2 | async-start | bytes 15728640 | tf_op jit(solution)/shard_map/all_gather | solution.py:16
  7.9 206.2 %reduce-scatter.2.cloned.1.call-start = ((), (), s32[]{:S(2)}) async-start(), calls=%async_computation.3 | async-start | bytes 1769472 | tf_op jit(solution)/shard_map/reduce_scatter | solution.py:31
  8.2 8.9 %collective-permute-start = (bf16[128,384]{0,1:T(8,128)(2,1)S(1)}, bf16[128,384]{0,1:T(8,128)(2,1)S(1)}, u32[]{:S(2)}, u32[]{:S(2)}) collective-permute-start(bf16[128,384]{0,1:T(8,128)(2,1)S(1)} %copy.6), channel_id=1, source_target_pairs={{0,1},{1,2},{2,3},{3,4},{4,5},{5,6},{6,7},{7,0},{8,9},{9,10},{10,1... | collective-permute-start | bytes 294920 | tf_op jit(solution)/shard_map/ppermute | solution.py:10
  17.1 7.3 %collective-permute-start.1 = (bf16[128,384]{0,1:T(8,128)(2,1)S(1)}, bf16[128,384]{0,1:T(8,128)(2,1)S(1)}, u32[]{:S(2)}, u32[]{:S(2)}) collective-permute-start(bf16[128,384]{0,1:T(8,128)(2,1)S(1)} %collective-permute-done), channel_id=1, source_target_pairs={{0,1},{1,2},{2,3},{3,4},{4,5},{5,6},{6,7},{7,0},{8,9},{9,10},{10,1... | collective-permute-start | bytes 294920 | tf_op jit(solution)/shard_map/ppermute | solution.py:10
  24.4 7.3 %collective-permute-start.2 = (bf16[128,384]{0,1:T(8,128)(2,1)S(1)}, bf16[128,384]{0,1:T(8,128)(2,1)S(1)}, u32[]{:S(2)}, u32[]{:S(2)}) collective-permute-start(bf16[128,384]{0,1:T(8,128)(2,1)S(1)} %collective-permute-done.1), channel_id=1, source_target_pairs={{0,1},{1,2},{2,3},{3,4},{4,5},{5,6},{6,7},{7,0},{8,9},{9,10},{10,1... | collective-permute-start | bytes 294920 | tf_op jit(solution)/shard_map/ppermute | solution.py:10
  31.7 7.3 %collective-permute-start.3 = (bf16[128,384]{0,1:T(8,128)(2,1)S(1)}, bf16[128,384]{0,1:T(8,128)(2,1)S(1)}, u32[]{:S(2)}, u32[]{:S(2)}) collective-permute-start(bf16[128,384]{0,1:T(8,128)(2,1)S(1)} %collective-permute-done.2), channel_id=1, source_target_pairs={{0,1},{1,2},{2,3},{3,4},{4,5},{5,6},{6,7},{7,0},{8,9},{9,10},{10,1... | collective-permute-start | bytes 294920 | tf_op jit(solution)/shard_map/ppermute | solution.py:10
  39.0 7.4 %collective-permute-start.4 = (bf16[128,384]{0,1:T(8,128)(2,1)S(1)}, bf16[128,384]{0,1:T(8,128)(2,1)S(1)}, u32[]{:S(2)}, u32[]{:S(2)}) collective-permute-start(bf16[128,384]{0,1:T(8,128)(2,1)S(1)} %collective-permute-done.3), channel_id=1, source_target_pairs={{0,1},{1,2},{2,3},{3,4},{4,5},{5,6},{6,7},{7,0},{8,9},{9,10},{10,1... | collective-permute-start | bytes 294920 | tf_op jit(solution)/shard_map/ppermute | solution.py:10
  46.4 8.2 %collective-permute-start.5 = (bf16[128,384]{0,1:T(8,128)(2,1)S(1)}, bf16[128,384]{0,1:T(8,128)(2,1)S(1)}, u32[]{:S(2)}, u32[]{:S(2)}) collective-permute-start(bf16[128,384]{0,1:T(8,128)(2,1)S(1)} %collective-permute-done.4), channel_id=1, source_target_pairs={{0,1},{1,2},{2,3},{3,4},{4,5},{5,6},{6,7},{7,0},{8,9},{9,10},{10,1... | collective-permute-start | bytes 294920 | tf_op jit(solution)/shard_map/ppermute | solution.py:10
  54.6 7.3 %collective-permute-start.6 = (bf16[128,384]{0,1:T(8,128)(2,1)S(1)}, bf16[128,384]{0,1:T(8,128)(2,1)S(1)}, u32[]{:S(2)}, u32[]{:S(2)}) collective-permute-start(bf16[128,384]{0,1:T(8,128)(2,1)S(1)} %collective-permute-done.5), channel_id=1, source_target_pairs={{0,1},{1,2},{2,3},{3,4},{4,5},{5,6},{6,7},{7,0},{8,9},{9,10},{10,1... | collective-permute-start | bytes 294920 | tf_op jit(solution)/shard_map/ppermute | solution.py:10
  62.5 59.7 %copy-start.2 = (s32[128]{0:T(128)S(1)}, s32[128]{0:T(128)}, u32[]{:S(2)}) copy-start(s32[128]{0:T(128)} %param.5) | copy-start | bytes 1540
  140.1 10.2 %copy-start = (bf16[128,2048]{1,0:T(8,128)(2,1)}, bf16[128,2048]{1,0:T(8,128)(2,1)S(1)}, u32[]{:S(2)}) copy-start(bf16[128,2048]{1,0:T(8,128)(2,1)S(1)} %fusion.2) | copy-start | bytes 1572868
  150.3 86.8 %all-gather.5.cloned.1.call-start = ((), (), s32[]{:S(2)}) async-start(), calls=%async_computation.4 | async-start | bytes 2621440 | tf_op jit(solution)/shard_map/all_gather | solution.py:34
Sparse Core Ops, SparseCore 0:
  9.5 84.7 all-gather.2
  150.4 63.6 reduce-scatter.1
  215.7 21.3 all-gather.4
